TPU v7x, 32 devices: a whole 2x2x4 slice. The times are simulated.
32 devices in a mesh: groups: 2 (over y), expert: 4 (over z), dp: 2 (over core), tensor: 2 (over x).
Axes of the slice: x: 2, y: 2, z: 4, core: 2. Of those that a mesh axis runs over, the one named last changes fastest.
Arguments:
- tokens: bfloat16 [2, 2048, 2048], P('dp', ('groups', 'expert', 'tensor')), parts along dimension 1, may hold values from -6 to 6
- proj_weight: bfloat16 [4, 2048, 3584], P('expert', 'dp', 'tensor'), may hold values from -0.125 to 0.125
- slot_grads: bfloat16 [2, 4, 32, 3584], P('dp', 'expert', 'groups', 'tensor'), parts along dimension 2, may hold values from -1.5 to 1.5
- gate_weights: float32 [2, 2, 32], P('dp', None, 'groups'), parts along dimension 2, may hold values from 0.2 to 1
- selected: int32 [2, 2, 32], P('dp', None, 'groups'), parts along dimension 2, may hold values from 0 to 1023, as said below
Outputs:
- token_grads: bfloat16 [2, 2048, 2048], P('dp', ('groups', 'expert', 'tensor')), parts along dimension 1
- weight_grads: bfloat16 [8, 2048, 3584], P(('groups', 'expert'), 'dp', 'tensor'), parts along dimension 0
There are 2 independent parts, one for each index of `groups`. A program takes and returns all parts, laid end to end along the dimension named above; an argument that names none is the same for every part. Nothing has to cross between parts.
Inputs may be any that keep to these rules, and one draw needn't show every extreme that they name: `selected`: each entry names a token of its own group. Within one group and one expert the 16 entries are distinct. In each group an expert takes at most 4 tokens from the 128 tokens of one device (tokens k * 128 to (k + 1) * 128 - 1), and exactly 4 from some devices.
All inputs are finite; a program needn't handle non-finite values.
Results may differ from a plain program's by a relative error of at most 0.011.
Values may be sent and summed in bfloat16 or wider, within the bound.
No kernel may reach another device: no remote copies, remote signals or barrier semaphores. Data moves between devices by JAX's collectives and lax.ppermute only.
A program may use at most 64 MiB of HBM per device.

v0:
```python
import jax
import jax.numpy as jnp
from jax import lax
from jax.sharding import PartitionSpec as P

MOST = 4


def local(tokens, proj_weight, slot_grads, gate_weights, selected):
    n_tensor = lax.axis_size("tensor")
    n_expert = lax.axis_size("expert")
    n_data = lax.axis_size("dp")
    owners = n_expert * n_tensor
    own_expert = lax.axis_index("expert")
    own_owner = own_expert * n_tensor + lax.axis_index("tensor")
    token_rows = tokens[0]
    tok_dev = token_rows.shape[0]
    features = token_rows.shape[1]
    chosen = selected[0]
    experts = chosen.shape[0]
    capacity = chosen.shape[1]
    owner_of = chosen // tok_dev
    local_row = chosen % tok_dev
    slot_ids = jnp.arange(capacity)
    earlier = slot_ids[None, :] < slot_ids[:, None]
    same_owner = owner_of[:, :, None] == owner_of[:, None, :]
    arrival = jnp.sum(same_owner & earlier[None], axis=2)
    slot_pos = jnp.arange(MOST)
    local_hits = owner_of == own_owner
    selector = local_hits[:, None, :] & (arrival[:, None, :] == slot_pos[None, :, None])
    filled = jnp.any(selector, axis=2)
    send_row = jnp.sum(jnp.where(selector, local_row[:, None, :], 0), axis=2)
    outgoing = jnp.where(filled[..., None], token_rows[send_row], jnp.zeros((), jnp.bfloat16))
    outgoing_all = jnp.broadcast_to(outgoing[:, None, None], (experts, 2, n_tensor, MOST, features))
    incoming = lax.all_to_all(
        outgoing_all.reshape(owners, MOST, features),
        ("expert", "tensor"),
        split_axis=0,
        concat_axis=0,
        tiled=True,
    )
    incoming = incoming.reshape(owners * MOST, features)
    own_index = own_expert // 2
    own_owners = lax.dynamic_index_in_dim(owner_of, own_index, 0, keepdims=False)
    own_arrival = lax.dynamic_index_in_dim(arrival, own_index, 0, keepdims=False)
    slot_rows = incoming[own_owners * MOST + own_arrival]
    gate_row = lax.dynamic_index_in_dim(gate_weights[0], own_index, 0, keepdims=False)
    scaled = (gate_row[:, None] * slot_grads[0, 0].astype(jnp.float32)).astype(jnp.bfloat16)
    partial_value_sum = lax.dot_general(
        scaled,
        lax.all_gather(proj_weight, "dp", axis=1, tiled=True)[0],
        (((1,), (1,)), ((), ())),
        preferred_element_type=jnp.float32,
    ).astype(jnp.bfloat16)
    slot_equal_mask = (own_owners[None, None, :] == jnp.arange(owners)[:, None, None]) & (
        own_arrival[None, None, :] == slot_pos[None, :, None]
    )
    slot_used = jnp.any(slot_equal_mask, axis=2)
    slot_index = jnp.sum(jnp.where(slot_equal_mask, slot_ids[None, None, :], 0), axis=2)
    returning = jnp.where(
        slot_used[..., None], partial_value_sum[slot_index], jnp.zeros((), jnp.bfloat16)
    )
    arrived = lax.all_to_all(
        returning, ("expert", "tensor"), split_axis=0, concat_axis=0, tiled=True
    )
    arrived = arrived.reshape(owners * MOST, features)
    complete_row = jnp.broadcast_to(send_row[:, None, None], (experts, 2, n_tensor, MOST)).reshape(
        owners * MOST
    )
    used_full = jnp.broadcast_to(filled[:, None, None], (experts, 2, n_tensor, MOST)).reshape(
        owners * MOST
    )
    placement = (jnp.arange(tok_dev)[:, None] == complete_row[None, :]) & used_full[None, :]
    token_grads = jnp.dot(
        placement.astype(jnp.bfloat16), arrived, preferred_element_type=jnp.float32
    )
    token_grads = token_grads.astype(jnp.bfloat16)[None]
    column_share = lax.all_to_all(slot_rows, "dp", split_axis=1, concat_axis=0, tiled=True)
    scaled_all = lax.all_gather(scaled, "dp", axis=0, tiled=True)
    column_share = column_share.reshape(n_data, capacity, column_share.shape[1])
    scaled_all = scaled_all.reshape(n_data, capacity, scaled_all.shape[1])
    per_group = jnp.einsum(
        "gcd,gcf->gdf", column_share, scaled_all, preferred_element_type=jnp.float32
    )
    per_group = per_group.astype(jnp.bfloat16).astype(jnp.float32)
    weight_grads = jnp.sum(per_group, axis=0).astype(jnp.bfloat16)[None]
    return (token_grads, weight_grads)


def solution(mesh):
    in_specs = (
        P("dp", ("groups", "expert", "tensor"), None),
        P("expert", "dp", "tensor"),
        P("dp", "expert", "groups", "tensor"),
        P("dp", None, "groups"),
        P("dp", None, "groups"),
    )
    out_specs = (
        P("dp", ("groups", "expert", "tensor"), None),
        P(("groups", "expert"), "dp", "tensor"),
    )
    return jax.shard_map(local, mesh=mesh, in_specs=in_specs, out_specs=out_specs, check_vma=False)
```

profile of v0, /device:TPU:0, one launch (start us, length us, event | category | flops | bytes accessed | tf_op | source)
XLA Modules:
  0.0 58.4 jit_solution(3440165395489555670)
XLA Ops:
  7.2 0.7 %all-gather.2.cloned.1.call-update = ((bf16[1,1024,1792]{2,1,0:T(8,128)(2,1)}), bf16[1,2048,1792]{2,1,0:T(8,128)(2,1)}) async-update(((), (), s32[]{:S(2)}) %all-gather.2.cloned.1.call-start, bf16[1,1024,1792]{2,1,0:T(8,128)(2,1)} %param.6) | async-update | bytes 14680088
  7.9 0.7 %broadcast_compare_fusion = (pred[2,16]{1,0:T(4,128)(4,1)S(1)}, s32[2,16]{1,0:T(2,128)S(1)}) fusion(s32[]{:T(128)S(6)} %add.79, s32[1,2,16]{2,1,0:T(2,128)} %param.9), kind=kLoop, calls=%fused_computation.53 | loop fusion | flops 512 | bytes 292 | tf_op jit(solution)/shard_map/eq | solution.py:29
  8.6 0.2 convert_reduce_fusion.1
  8.8 0.7 %and_select_fusion.1 = s32[2,16]{1,0:T(2,128)S(1)} fusion(s32[1,2,16]{2,1,0:T(2,128)} %param.9), kind=kLoop, calls=%fused_computation.41 | loop fusion | flops 352 | bytes 256 | tf_op jit(solution)/shard_map/jit(remainder)/select_n | solution.py:23
  9.5 0.1 select_reduce_fusion
  9.7 0.1 reshape.265
  9.8 0.6 gather_fusion.1
  10.4 0.2 fusion.19
  10.5 0.1 broadcast_select_fusion.1
  10.6 0.7 %broadcast_in_dim.104 = bf16[2,2,2,4,2048]{4,3,2,1,0:T(4,128)(2,1)} broadcast(bf16[2,4,2048]{2,1,0:T(4,128)(2,1)S(1)} %broadcast_select_fusion.1), dimensions={0,3,4} | broadcast | bytes 163840 | tf_op jit(solution)/shard_map/broadcast_in_dim | solution.py:34
  11.3 7.3 %all-to-all-start.1 = ((bf16[8,4,2048]{2,1,0:T(4,128)(2,1)}), bf16[8,4,2048]{2,1,0:T(4,128)(2,1)S(1)}, u32[]{:S(2)}, u32[]{:S(2)}) async-start(bf16[8,4,2048]{2,1,0:T(4,128)(2,1)} %bitcast.10), calls=%async_computation.1 | async-start | bytes 262144 | tf_op jit(solution)/shard_map/all_to_all | solution.py:35
  18.6 0.7 %fusion.20 = f32[16]{0:T(128)S(1)} fusion(f32[1,2,16]{2,1,0:T(2,128)} %param.8, s32[]{:T(128)S(6)} %select_n.92), kind=kLoop, calls=%fused_computation.51 | loop fusion | bytes 132 | tf_op jit(solution)/shard_map/jit(dynamic_index_in_dim)/dynamic_slice | solution.py:47
  19.3 0.2 and_reduce_fusion
  19.5 0.2 fusion.17
  19.6 0.9 %fusion.8 = bf16[16,1792]{1,0:T(8,128)(2,1)S(1)} fusion(bf16[1,1,16,1792]{3,2,1,0:T(8,128)(2,1)} %param.7, f32[16]{0:T(128)S(1)} %fusion.20), kind=kLoop, calls=%fused_computation.14 | loop fusion | flops 86016 | bytes 114752 | tf_op jit(solution)/shard_map/convert_element_type | solution.py:48
  20.5 0.1 copy.10
  20.6 0.1 copy.11
  20.7 0.1 reshape.257
  20.8 0.1 and.91
  20.9 0.1 eq.100
  21.0 4.9 %all-to-all-done.1 = bf16[8,4,2048]{2,1,0:T(4,128)(2,1)S(1)} async-done(((bf16[8,4,2048]{2,1,0:T(4,128)(2,1)}), bf16[8,4,2048]{2,1,0:T(4,128)(2,1)S(1)}, u32[]{:S(2)}, u32[]{:S(2)}) %all-to-all-start.1) | async-done | bytes 131104 | tf_op jit(solution)/shard_map/all_to_all | solution.py:35
  26.0 0.6 %gather_fusion.2 = bf16[16,2048]{1,0:T(8,128)(2,1)S(1)} fusion(bf16[32,2048]{1,0:T(8,128)(2,1)S(1)} %reshape.252, s32[1024]{0:T(1024)S(1)} %pad_clamp_fusion), kind=kCustom, calls=%fused_computation.2 | custom fusion | bytes 131136 | tf_op jit(solution)/shard_map/gather | solution.py:46
  26.6 0.6 %copy.15 = bf16[2,2,8,1024]{3,2,0,1:T(8,128)(2,1)} copy(bf16[2,2,8,1024]{3,2,1,0:T(8,128)(2,1)S(1)} %bitcast.71) | data formatting | bytes 131072 | tf_op jit(solution)/shard_map/all_to_all | solution.py:78
  27.2 3.3 %all-to-all-start.2 = ((bf16[16,2,1024]{2,0,1:T(8,128)(2,1)}), bf16[16,2,1024]{2,0,1:T(8,128)(2,1)S(1)}, u32[]{:S(2)}, u32[]{:S(2)}) async-start(bf16[16,2,1024]{2,0,1:T(8,128)(2,1)} %bitcast.67), calls=%async_computation.2 | async-start | bytes 131072 | tf_op jit(solution)/shard_map/all_to_all | solution.py:78
  30.6 5.1 %fusion.3 = bf16[16,2048]{1,0:T(8,128)(2,1)S(1)} fusion(bf16[1,2048,1792]{2,1,0:T(8,128)(2,1)} %all-gather.2.cloned.1.call-done, bf16[1,1,16,1792]{3,2,1,0:T(8,128)(2,1)} %param.7, f32[16]{0:T(128)S(1)} %fusion.20), kind=kOutput, calls=%fused_computation.8 | convolution fusion | flops 117559296 | bytes 7462976 | tf_op jit(solution)/shard_map/dot_general | solution.py:49
  35.7 0.7 %gather_fusion = bf16[32,2048]{1,0:T(8,128)(2,1)S(1)} fusion(bf16[16,2048]{1,0:T(8,128)(2,1)S(1)} %fusion.3, s32[1024]{0:T(1024)S(1)} %pad_clamp_fusion.2), kind=kCustom, calls=%fused_computation | custom fusion | bytes 262272 | tf_op jit(solution)/shard_map/gather | solution.py:61
  36.4 0.8 %broadcast_select_fusion = bf16[8,4,2048]{2,1,0:T(4,128)(2,1)} fusion(bf16[8,4,2048]{2,1,0:T(4,128)(2,1)S(1)} %reshape.256, pred[8,4]{1,0:T(8,128)(4,1)S(1)} %copy.10), kind=kLoop, calls=%fused_computation.11 | loop fusion | flops 65536 | bytes 262176 | tf_op jit(solution)/shard_map/jit(_where)/select_n | solution.py:60
  37.2 5.8 %all-to-all-start = ((bf16[8,4,2048]{2,1,0:T(4,128)(2,1)}), bf16[8,4,2048]{2,1,0:T(4,128)(2,1)S(1)}, u32[]{:S(2)}, u32[]{:S(2)}) async-start(bf16[8,4,2048]{2,1,0:T(4,128)(2,1)} %broadcast_select_fusion), calls=%async_computation | async-start | bytes 262144 | tf_op jit(solution)/shard_map/all_to_all | solution.py:63
  43.0 1.9 %all_gather.7 = bf16[32,1792]{1,0:T(8,128)(2,1)S(1)} all-gather(bf16[16,1792]{1,0:T(8,128)(2,1)S(1)} %fusion.8), channel_id=1, replica_groups=mesh['groups'=2,'expert'=4,'dp'=2,'tensor'=2] {'dp'}, dimensions={0}, use_global_device_ids=true | all-gather | bytes 172032 | tf_op jit(solution)/shard_map/all_gather | solution.py:79
  44.9 4.3 %convert_reduce_fusion = bf16[1024,1792]{1,0:T(8,128)(2,1)} fusion(bf16[2,16,1792]{2,1,0:T(8,128)(2,1)S(1)} %bitcast.70, bf16[16,2,1024]{2,0,1:T(8,128)(2,1)S(1)} %all-to-all-done.2), kind=kOutput, calls=%fused_computation.5 | convolution fusion | flops 122945536 | bytes 3850240 | tf_op jit(solution)/shard_map/gcd,gcf->gdf/dot_general | solution.py:82
  49.2 1.3 %all-to-all-done = bf16[8,4,2048]{2,1,0:T(4,128)(2,1)S(1)} async-done(((bf16[8,4,2048]{2,1,0:T(4,128)(2,1)}), bf16[8,4,2048]{2,1,0:T(4,128)(2,1)S(1)}, u32[]{:S(2)}, u32[]{:S(2)}) %all-to-all-start) | async-done | bytes 131104 | tf_op jit(solution)/shard_map/all_to_all | solution.py:63
  50.5 1.1 %fusion.2 = bf16[1,128,2048]{2,1,0:T(8,128)(2,1)} fusion(bf16[32,2048]{1,0:T(8,128)(2,1)S(1)} %reshape.250, s32[32]{0:T(128)S(1)} %eq.100, pred[32]{0:T(512)(128)(4,1)S(1)} %and.91), kind=kOutput, calls=%fused_computation.7 | convolution fusion | flops 17047552 | bytes 655520 | tf_op jit(solution)/shard_map/dot_general | solution.py:74
  (21 shorter events, 0.4 us)
Async XLA Ops:
  7.2 2.6 %copy-start = (bf16[1,128,2048]{2,1,0:T(8,128)(2,1)S(1)}, bf16[1,128,2048]{2,1,0:T(8,128)(2,1)}, u32[]{:S(2)}) copy-start(bf16[1,128,2048]{2,1,0:T(8,128)(2,1)} %param.5) | copy-start | bytes 1572868
  7.2 23.4 %all-gather.2.cloned.1.call-start = ((), (), s32[]{:S(2)}) async-start(), calls=%async_computation.3 | async-start | bytes 11010048 | tf_op jit(solution)/shard_map/all_gather | solution.py:51
  11.3 14.6 %all-to-all-start.1 = ((bf16[8,4,2048]{2,1,0:T(4,128)(2,1)}), bf16[8,4,2048]{2,1,0:T(4,128)(2,1)S(1)}, u32[]{:S(2)}, u32[]{:S(2)}) async-start(bf16[8,4,2048]{2,1,0:T(4,128)(2,1)} %bitcast.10), calls=%async_computation.1 | async-start | bytes 262144 | tf_op jit(solution)/shard_map/all_to_all | solution.py:35
  27.2 10.0 %all-to-all-start.2 = ((bf16[16,2,1024]{2,0,1:T(8,128)(2,1)}), bf16[16,2,1024]{2,0,1:T(8,128)(2,1)S(1)}, u32[]{:S(2)}, u32[]{:S(2)}) async-start(bf16[16,2,1024]{2,0,1:T(8,128)(2,1)} %bitcast.67), calls=%async_computation.2 | async-start | bytes 131072 | tf_op jit(solution)/shard_map/all_to_all | solution.py:78
  37.2 13.3 %all-to-all-start = ((bf16[8,4,2048]{2,1,0:T(4,128)(2,1)}), bf16[8,4,2048]{2,1,0:T(4,128)(2,1)S(1)}, u32[]{:S(2)}, u32[]{:S(2)}) async-start(bf16[8,4,2048]{2,1,0:T(4,128)(2,1)} %broadcast_select_fusion), calls=%async_computation | async-start | bytes 262144 | tf_op jit(solution)/shard_map/all_to_all | solution.py:63
Sparse Core Ops, SparseCore 0:
  9.5 21.0 all-gather.1
where the time goes:
time: 59 us; the launch traced here: 58.4 us
  starting transfers between devices  16.4 us (28%)
  between operations  14.1 us (24%)
  matrix products  10.5 us (18%)
  waiting for transfers between devices  6.92 us (12%)
  local copies, waits for them, and re-layouts  4.56 us (8%)
  other arithmetic  4.02 us (7%)
  blocking collectives  1.88 us (3%)
    all_to_all x1, starting transfers between devices, local(): lax.all_to_all(outgoing_all.reshape(owners, MOST, features), ('expert', '...  7.28 us
    all_to_all x1, starting transfers between devices, local(): lax.all_to_all(returning, ('expert', 'tensor'), split_axis=0, concat_axis...  5.83 us
    dot_general x1, matrix products, local(): lax.dot_general(scaled, lax.all_gather(proj_weight, 'dp', axis=1, tiled=T...  5.11 us
    all_to_all x1, waiting for transfers between devices, local(): lax.all_to_all(outgoing_all.reshape(owners, MOST, features), ('expert', '...  4.91 us
    dot_general x1, matrix products, local(): jnp.einsum('gcd,gcf->gdf', column_share, scaled_all, preferred_element_ty...  4.31 us
    all_to_all x1, starting transfers between devices, local(): lax.all_to_all(slot_rows, 'dp', split_axis=1, concat_axis=0, tiled=True)  3.3 us
    all_gather x1, blocking collectives, local(): scaled_all = lax.all_gather(scaled, 'dp', axis=0, tiled=True)  1.88 us
    all_to_all x1, waiting for transfers between devices, local(): lax.all_to_all(returning, ('expert', 'tensor'), split_axis=0, concat_axis...  1.25 us
  transfers between devices with their start and end apart: 4, of which 3 were waited for; matrix products, arithmetic and copies ran while one was open for 31% of the time, Pallas kernels for 0%

commit v1 on v0

--- a/solution.py
+++ b/solution.py
@@ -4,6 +4,17 @@
 from jax.sharding import PartitionSpec as P
 
 MOST = 4
+
+
+def cut_along(array, dim, size):
+    before, after = (array.shape[:dim], array.shape[dim + 1 :])
+    return jnp.moveaxis(array.reshape(*before, size, -1, *after), dim, 0)
+
+
+def laid_out(tiles, dim):
+    shape = list(tiles.shape[1:])
+    shape[dim] *= tiles.shape[0]
+    return jnp.moveaxis(tiles, 0, dim).reshape(shape)
 
 
 def local(tokens, proj_weight, slot_grads, gate_weights, selected):
@@ -32,13 +43,18 @@
     send_row = jnp.sum(jnp.where(selector, local_row[:, None, :], 0), axis=2)
     outgoing = jnp.where(filled[..., None], token_rows[send_row], jnp.zeros((), jnp.bfloat16))
     outgoing_all = jnp.broadcast_to(outgoing[:, None, None], (experts, 2, n_tensor, MOST, features))
-    incoming = lax.all_to_all(
-        outgoing_all.reshape(owners, MOST, features),
-        ("expert", "tensor"),
-        split_axis=0,
-        concat_axis=0,
-        tiled=True,
-    )
+    value = outgoing_all.reshape(owners, MOST, features)
+    size, place = (lax.axis_size(("expert", "tensor")), lax.axis_index(("expert", "tensor")))
+    blocks = cut_along(value, 0, size)
+    out = blocks
+    for turn in range(1, size):
+        target, source = ((place + turn) % size, (place - turn) % size)
+        sent = lax.dynamic_index_in_dim(blocks, target, 0)
+        partner_block = lax.ppermute(
+            sent, ("expert", "tensor"), [(i, (i + turn) % size) for i in range(size)]
+        )
+        out = lax.dynamic_update_slice_in_dim(out, partner_block, source, axis=0)
+    incoming = laid_out(out, 0)
     incoming = incoming.reshape(owners * MOST, features)
     own_index = own_expert // 2
     own_owners = lax.dynamic_index_in_dim(owner_of, own_index, 0, keepdims=False)

time: 59 us -> 62.2 us (1.054)
  starting transfers between devices: 16.4 us -> 19.1 us
  waiting for transfers between devices: 6.92 us -> 7.72 us
    ppermute x0 -> x7, starting transfers between devices: none -> 11.3 us  [local(): lax.ppermute(sent, ('expert', 'tensor'), [(i, (i + turn) % size) for i in...]
    all_to_all x1 -> x0, starting transfers between devices: 7.28 us -> none  [local(): lax.all_to_all(outgoing_all.reshape(owners, MOST, features), ('expert', '...]
    ppermute x0 -> x7, waiting for transfers between devices: none -> 5.59 us  [local(): lax.ppermute(sent, ('expert', 'tensor'), [(i, (i + turn) % size) for i in...]
    all_to_all x1 -> x0, waiting for transfers between devices: 4.91 us -> none  [local(): lax.all_to_all(outgoing_all.reshape(owners, MOST, features), ('expert', '...]
    all_to_all x1, starting transfers between devices: 5.83 us -> 4.54 us  [local(): lax.all_to_all(returning, ('expert', 'tensor'), split_axis=0, concat_axis...]
    broadcast_in_dim x1, local copies, waits for them, and re-layouts: 0.69 us -> 0.04 us  [local(): jnp.broadcast_to(outgoing[:, None, None], (experts, 2, n_tensor, MOST, fe...]
  transfers between devices with their start and end apart: 4 -> 10, of which waited for: 3 -> 4; matrix products, arithmetic and copies ran while one was open for 31% -> 28% of each run, Pallas kernels for 0% -> 0%
where the time goes in v1:
time: 62.2 us; the launch traced here: 61.7 us
  starting transfers between devices  19.1 us (31%)
  between operations  14.4 us (23%)
  matrix products  10.5 us (17%)
  waiting for transfers between devices  7.72 us (12%)
  local copies, waits for them, and re-layouts  4.07 us (7%)
  other arithmetic  4 us (6%)
  blocking collectives  1.88 us (3%)
    ppermute x7, starting transfers between devices, local(): lax.ppermute(sent, ('expert', 'tensor'), [(i, (i + turn) % size) for i in...  11.3 us
    ppermute x7, waiting for transfers between devices, local(): lax.ppermute(sent, ('expert', 'tensor'), [(i, (i + turn) % size) for i in...  5.59 us
    dot_general x1, matrix products, local(): lax.dot_general(scaled, lax.all_gather(proj_weight, 'dp', axis=1, tiled=T...  5.11 us
    all_to_all x1, starting transfers between devices, local(): lax.all_to_all(returning, ('expert', 'tensor'), split_axis=0, concat_axis...  4.54 us
    dot_general x1, matrix products, local(): jnp.einsum('gcd,gcf->gdf', column_share, scaled_all, preferred_element_ty...  4.31 us
    all_to_all x1, starting transfers between devices, local(): lax.all_to_all(slot_rows, 'dp', split_axis=1, concat_axis=0, tiled=True)  3.3 us
    all_gather x1, blocking collectives, local(): scaled_all = lax.all_gather(scaled, 'dp', axis=0, tiled=True)  1.88 us
    all_to_all x1, waiting for transfers between devices, local(): lax.all_to_all(returning, ('expert', 'tensor'), split_axis=0, concat_axis...  1.43 us
  transfers between devices with their start and end apart: 10, of which 4 were waited for; matrix products, arithmetic and copies ran while one was open for 28% of the time, Pallas kernels for 0%

profile of v1, /device:TPU:0, one launch (start us, length us, event | category | flops | bytes accessed | tf_op | source)
XLA Modules:
  0.0 61.7 jit_solution(505792765544632029)
XLA Ops:
  7.2 0.7 %all-gather.2.cloned.1.call-update = ((bf16[1,1024,1792]{2,1,0:T(8,128)(2,1)}), bf16[1,2048,1792]{2,1,0:T(8,128)(2,1)}) async-update(((), (), s32[]{:S(2)}) %all-gather.2.cloned.1.call-start, bf16[1,1024,1792]{2,1,0:T(8,128)(2,1)} %param.6) | async-update | bytes 14680088
  7.9 0.7 %broadcast_compare_fusion = (pred[2,16]{1,0:T(4,128)(4,1)S(1)}, s32[2,16]{1,0:T(2,128)S(1)}) fusion(s32[]{:T(128)S(6)} %add.194, s32[1,2,16]{2,1,0:T(2,128)} %param.9), kind=kLoop, calls=%fused_computation.67 | loop fusion | flops 512 | bytes 292 | tf_op jit(solution)/shard_map/eq | solution.py:40
  8.6 0.2 convert_reduce_fusion.1
  8.8 0.7 %and_select_fusion.1 = s32[2,16]{1,0:T(2,128)S(1)} fusion(s32[1,2,16]{2,1,0:T(2,128)} %param.9), kind=kLoop, calls=%fused_computation.58 | loop fusion | flops 352 | bytes 256 | tf_op jit(solution)/shard_map/jit(remainder)/select_n | solution.py:34
  9.5 0.1 select_reduce_fusion
  9.8 0.6 gather_fusion.1
  10.4 0.2 fusion.19
  10.7 3.0 %collective-permute-start = (bf16[1,1,4,2048]{3,2,0,1:T(4,128)(2,1)S(1)}, bf16[1,1,4,2048]{3,2,0,1:T(4,128)(2,1)S(1)}, u32[]{:S(2)}, u32[]{:S(2)}) collective-permute-start(bf16[1,1,4,2048]{3,2,0,1:T(4,128)(2,1)S(1)} %constant_dynamic-slice_fusion.6), channel_id=1, source_target_pairs={{0,1},{1,4},{4,5},{5,8},{8,9},{9,12},{12,13},{13,0},{2,3},{3,6},{6... | collective-permute-start | bytes 49160 | tf_op jit(solution)/shard_map/ppermute | solution.py:53
  13.7 0.1 fusion.17
  14.1 0.7 %fusion.21 = f32[16]{0:T(128)S(1)} fusion(f32[1,2,16]{2,1,0:T(2,128)} %param.8, s32[]{:T(128)S(6)} %select_n.193), kind=kLoop, calls=%fused_computation.66 | loop fusion | bytes 132 | tf_op jit(solution)/shard_map/jit(dynamic_index_in_dim)/dynamic_slice | solution.py:63
  14.8 0.2 and_reduce_fusion
  14.9 0.9 %fusion.8 = bf16[16,1792]{1,0:T(8,128)(2,1)S(1)} fusion(bf16[1,1,16,1792]{3,2,1,0:T(8,128)(2,1)} %param.7, f32[16]{0:T(128)S(1)} %fusion.21), kind=kLoop, calls=%fused_computation.14 | loop fusion | flops 86016 | bytes 114752 | tf_op jit(solution)/shard_map/convert_element_type | solution.py:64
  15.9 2.5 %collective-permute-done = bf16[1,1,4,2048]{3,2,0,1:T(4,128)(2,1)S(1)} collective-permute-done((bf16[1,1,4,2048]{3,2,0,1:T(4,128)(2,1)S(1)}, bf16[1,1,4,2048]{3,2,0,1:T(4,128)(2,1)S(1)}, u32[]{:S(2)}, u32[]{:S(2)}) %collective-permute-start) | collective-permute-done | bytes 16416 | tf_op jit(solution)/shard_map/ppermute | solution.py:53
  18.7 0.1 copy.10
  19.0 1.5 %collective-permute-start.2 = (bf16[1,1,4,2048]{3,2,0,1:T(4,128)(2,1)S(1)}, bf16[1,1,4,2048]{3,2,0,1:T(4,128)(2,1)S(1)}, u32[]{:S(2)}, u32[]{:S(2)}) collective-permute-start(bf16[1,1,4,2048]{3,2,0,1:T(4,128)(2,1)S(1)} %get-tuple-element.8), channel_id=1, source_target_pairs={{0,5},{1,8},{4,9},{5,12},{8,13},{9,0},{12,1},{13,4},{2,7},{3,10},{... | collective-permute-start | bytes 49160 | tf_op jit(solution)/shard_map/ppermute | solution.py:53
  20.5 1.2 %collective-permute-start.3 = (bf16[1,1,4,2048]{3,2,0,1:T(4,128)(2,1)S(1)}, bf16[1,1,4,2048]{3,2,0,1:T(4,128)(2,1)S(1)}, u32[]{:S(2)}, u32[]{:S(2)}) collective-permute-start(bf16[1,1,4,2048]{3,2,0,1:T(4,128)(2,1)S(1)} %get-tuple-element.7), channel_id=1, source_target_pairs={{0,8},{1,9},{4,12},{5,13},{8,0},{9,1},{12,4},{13,5},{2,10},{3,11},... | collective-permute-start | bytes 49160 | tf_op jit(solution)/shard_map/ppermute | solution.py:53
  21.8 3.5 %collective-permute-start.4 = (bf16[1,1,4,2048]{3,2,0,1:T(4,128)(2,1)S(1)}, bf16[1,1,4,2048]{3,2,0,1:T(4,128)(2,1)S(1)}, u32[]{:S(2)}, u32[]{:S(2)}) collective-permute-start(bf16[1,1,4,2048]{3,2,0,1:T(4,128)(2,1)S(1)} %get-tuple-element.6), channel_id=1, source_target_pairs={{0,9},{1,12},{4,13},{5,0},{8,1},{9,4},{12,5},{13,8},{2,11},{3,14},... | collective-permute-start | bytes 49160 | tf_op jit(solution)/shard_map/ppermute | solution.py:53
  25.3 1.3 %collective-permute-start.5 = (bf16[1,1,4,2048]{3,2,0,1:T(4,128)(2,1)S(1)}, bf16[1,1,4,2048]{3,2,0,1:T(4,128)(2,1)S(1)}, u32[]{:S(2)}, u32[]{:S(2)}) collective-permute-start(bf16[1,1,4,2048]{3,2,0,1:T(4,128)(2,1)S(1)} %get-tuple-element.5), channel_id=1, source_target_pairs={{0,12},{1,13},{4,0},{5,1},{8,4},{9,5},{12,8},{13,9},{2,14},{3,15},... | collective-permute-start | bytes 49160 | tf_op jit(solution)/shard_map/ppermute | solution.py:53
  26.6 0.6 collective-permute-start.6
  27.3 1.7 %collective-permute-done.5 = bf16[1,1,4,2048]{3,2,0,1:T(4,128)(2,1)S(1)} collective-permute-done((bf16[1,1,4,2048]{3,2,0,1:T(4,128)(2,1)S(1)}, bf16[1,1,4,2048]{3,2,0,1:T(4,128)(2,1)S(1)}, u32[]{:S(2)}, u32[]{:S(2)}) %collective-permute-start.5) | collective-permute-done | bytes 16416 | tf_op jit(solution)/shard_map/ppermute | solution.py:53
  29.0 1.3 %collective-permute-done.6 = bf16[1,1,4,2048]{3,2,0,1:T(4,128)(2,1)S(1)} collective-permute-done((bf16[1,1,4,2048]{3,2,0,1:T(4,128)(2,1)S(1)}, bf16[1,1,4,2048]{3,2,0,1:T(4,128)(2,1)S(1)}, u32[]{:S(2)}, u32[]{:S(2)}) %collective-permute-start.6) | collective-permute-done | bytes 16416 | tf_op jit(solution)/shard_map/ppermute | solution.py:53
  30.4 0.6 gather_fusion.2
  31.0 0.6 %copy.15 = bf16[2,2,8,1024]{3,2,0,1:T(8,128)(2,1)} copy(bf16[2,2,8,1024]{3,2,1,0:T(8,128)(2,1)S(1)} %bitcast.75) | data formatting | bytes 131072 | tf_op jit(solution)/shard_map/all_to_all | solution.py:94
  31.7 3.3 %all-to-all-start.1 = ((bf16[16,2,1024]{2,0,1:T(8,128)(2,1)}), bf16[16,2,1024]{2,0,1:T(8,128)(2,1)S(1)}, u32[]{:S(2)}, u32[]{:S(2)}) async-start(bf16[16,2,1024]{2,0,1:T(8,128)(2,1)} %bitcast.69), calls=%async_computation.1 | async-start | bytes 131072 | tf_op jit(solution)/shard_map/all_to_all | solution.py:94
  35.0 5.1 %fusion.3 = bf16[16,2048]{1,0:T(8,128)(2,1)S(1)} fusion(bf16[1,2048,1792]{2,1,0:T(8,128)(2,1)} %all-gather.2.cloned.1.call-done, bf16[1,1,16,1792]{3,2,1,0:T(8,128)(2,1)} %param.7, f32[16]{0:T(128)S(1)} %fusion.21), kind=kOutput, calls=%fused_computation.8 | convolution fusion | flops 117559296 | bytes 7462976 | tf_op jit(solution)/shard_map/dot_general | solution.py:65
  40.1 0.7 %gather_fusion = bf16[32,2048]{1,0:T(8,128)(2,1)S(1)} fusion(bf16[16,2048]{1,0:T(8,128)(2,1)S(1)} %fusion.3, s32[1024]{0:T(1024)S(1)} %pad_clamp_fusion.2), kind=kCustom, calls=%fused_computation | custom fusion | bytes 262272 | tf_op jit(solution)/shard_map/gather | solution.py:77
  40.8 0.8 %broadcast_select_fusion = bf16[8,4,2048]{2,1,0:T(4,128)(2,1)} fusion(bf16[8,4,2048]{2,1,0:T(4,128)(2,1)S(1)} %reshape.248, pred[8,4]{1,0:T(8,128)(4,1)S(1)} %copy.10), kind=kLoop, calls=%fused_computation.11 | loop fusion | flops 65536 | bytes 262176 | tf_op jit(solution)/shard_map/jit(_where)/select_n | solution.py:76
  41.6 4.5 %all-to-all-start = ((bf16[8,4,2048]{2,1,0:T(4,128)(2,1)}), bf16[8,4,2048]{2,1,0:T(4,128)(2,1)S(1)}, u32[]{:S(2)}, u32[]{:S(2)}) async-start(bf16[8,4,2048]{2,1,0:T(4,128)(2,1)} %broadcast_select_fusion), calls=%async_computation | async-start | bytes 262144 | tf_op jit(solution)/shard_map/all_to_all | solution.py:79
  46.2 1.9 %all_gather.7 = bf16[32,1792]{1,0:T(8,128)(2,1)S(1)} all-gather(bf16[16,1792]{1,0:T(8,128)(2,1)S(1)} %fusion.8), channel_id=1, replica_groups=mesh['groups'=2,'expert'=4,'dp'=2,'tensor'=2] {'dp'}, dimensions={0}, use_global_device_ids=true | all-gather | bytes 172032 | tf_op jit(solution)/shard_map/all_gather | solution.py:95
  48.0 4.3 %convert_reduce_fusion = bf16[1024,1792]{1,0:T(8,128)(2,1)} fusion(bf16[2,16,1792]{2,1,0:T(8,128)(2,1)S(1)} %bitcast.74, bf16[16,2,1024]{2,0,1:T(8,128)(2,1)S(1)} %all-to-all-done.1), kind=kOutput, calls=%fused_computation.5 | convolution fusion | flops 122945536 | bytes 3850240 | tf_op jit(solution)/shard_map/gcd,gcf->gdf/dot_general | solution.py:98
  52.4 1.4 %all-to-all-done = bf16[8,4,2048]{2,1,0:T(4,128)(2,1)S(1)} async-done(((bf16[8,4,2048]{2,1,0:T(4,128)(2,1)}), bf16[8,4,2048]{2,1,0:T(4,128)(2,1)S(1)}, u32[]{:S(2)}, u32[]{:S(2)}) %all-to-all-start) | async-done | bytes 131104 | tf_op jit(solution)/shard_map/all_to_all | solution.py:79
  53.8 1.1 %fusion.2 = bf16[1,128,2048]{2,1,0:T(8,128)(2,1)} fusion(bf16[32,2048]{1,0:T(8,128)(2,1)S(1)} %reshape.244, s32[32]{0:T(128)S(1)} %eq.115, pred[32]{0:T(512)(128)(4,1)S(1)} %and.148), kind=kOutput, calls=%fused_computation.7 | convolution fusion | flops 17047552 | bytes 655520 | tf_op jit(solution)/shard_map/dot_general | solution.py:90
  (41 shorter events, 1.1 us)
Async XLA Ops:
  7.2 2.6 %copy-start = (bf16[1,128,2048]{2,1,0:T(8,128)(2,1)S(1)}, bf16[1,128,2048]{2,1,0:T(8,128)(2,1)}, u32[]{:S(2)}) copy-start(bf16[1,128,2048]{2,1,0:T(8,128)(2,1)} %param.5) | copy-start | bytes 1572868
  7.2 27.8 %all-gather.2.cloned.1.call-start = ((), (), s32[]{:S(2)}) async-start(), calls=%async_computation.2 | async-start | bytes 11010048 | tf_op jit(solution)/shard_map/all_gather | solution.py:67
  10.7 7.8 %collective-permute-start = (bf16[1,1,4,2048]{3,2,0,1:T(4,128)(2,1)S(1)}, bf16[1,1,4,2048]{3,2,0,1:T(4,128)(2,1)S(1)}, u32[]{:S(2)}, u32[]{:S(2)}) collective-permute-start(bf16[1,1,4,2048]{3,2,0,1:T(4,128)(2,1)S(1)} %constant_dynamic-slice_fusion.6), channel_id=1, source_target_pairs={{0,1},{1,4},{4,5},{5,8},{8,9},{9,12},{12,13},{13,0},{2,3},{3,6},{6... | collective-permute-start | bytes 49160 | tf_op jit(solution)/shard_map/ppermute | solution.py:53
  18.5 8.1 %collective-permute-start.1 = (bf16[1,1,4,2048]{3,2,0,1:T(4,128)(2,1)S(1)}, bf16[1,1,4,2048]{3,2,0,1:T(4,128)(2,1)S(1)}, u32[]{:S(2)}, u32[]{:S(2)}) collective-permute-start(bf16[1,1,4,2048]{3,2,0,1:T(4,128)(2,1)S(1)} %get-tuple-element.9), channel_id=1, source_target_pairs={{0,4},{1,5},{4,8},{5,9},{8,12},{9,13},{12,0},{13,1},{2,6},{3,7},{6... | collective-permute-start | bytes 49160 | tf_op jit(solution)/shard_map/ppermute | solution.py:53
  19.0 8.2 %collective-permute-start.2 = (bf16[1,1,4,2048]{3,2,0,1:T(4,128)(2,1)S(1)}, bf16[1,1,4,2048]{3,2,0,1:T(4,128)(2,1)S(1)}, u32[]{:S(2)}, u32[]{:S(2)}) collective-permute-start(bf16[1,1,4,2048]{3,2,0,1:T(4,128)(2,1)S(1)} %get-tuple-element.8), channel_id=1, source_target_pairs={{0,5},{1,8},{4,9},{5,12},{8,13},{9,0},{12,1},{13,4},{2,7},{3,10},{... | collective-permute-start | bytes 49160 | tf_op jit(solution)/shard_map/ppermute | solution.py:53
  20.5 6.7 %collective-permute-start.3 = (bf16[1,1,4,2048]{3,2,0,1:T(4,128)(2,1)S(1)}, bf16[1,1,4,2048]{3,2,0,1:T(4,128)(2,1)S(1)}, u32[]{:S(2)}, u32[]{:S(2)}) collective-permute-start(bf16[1,1,4,2048]{3,2,0,1:T(4,128)(2,1)S(1)} %get-tuple-element.7), channel_id=1, source_target_pairs={{0,8},{1,9},{4,12},{5,13},{8,0},{9,1},{12,4},{13,5},{2,10},{3,11},... | collective-permute-start | bytes 49160 | tf_op jit(solution)/shard_map/ppermute | solution.py:53
  21.8 5.5 %collective-permute-start.4 = (bf16[1,1,4,2048]{3,2,0,1:T(4,128)(2,1)S(1)}, bf16[1,1,4,2048]{3,2,0,1:T(4,128)(2,1)S(1)}, u32[]{:S(2)}, u32[]{:S(2)}) collective-permute-start(bf16[1,1,4,2048]{3,2,0,1:T(4,128)(2,1)S(1)} %get-tuple-element.6), channel_id=1, source_target_pairs={{0,9},{1,12},{4,13},{5,0},{8,1},{9,4},{12,5},{13,8},{2,11},{3,14},... | collective-permute-start | bytes 49160 | tf_op jit(solution)/shard_map/ppermute | solution.py:53
  25.3 3.7 %collective-permute-start.5 = (bf16[1,1,4,2048]{3,2,0,1:T(4,128)(2,1)S(1)}, bf16[1,1,4,2048]{3,2,0,1:T(4,128)(2,1)S(1)}, u32[]{:S(2)}, u32[]{:S(2)}) collective-permute-start(bf16[1,1,4,2048]{3,2,0,1:T(4,128)(2,1)S(1)} %get-tuple-element.5), channel_id=1, source_target_pairs={{0,12},{1,13},{4,0},{5,1},{8,4},{9,5},{12,8},{13,9},{2,14},{3,15},... | collective-permute-start | bytes 49160 | tf_op jit(solution)/shard_map/ppermute | solution.py:53
  26.6 3.7 %collective-permute-start.6 = (bf16[1,1,4,2048]{3,2,0,1:T(4,128)(2,1)S(1)}, bf16[1,1,4,2048]{3,2,0,1:T(4,128)(2,1)S(1)}, u32[]{:S(2)}, u32[]{:S(2)}) collective-permute-start(bf16[1,1,4,2048]{3,2,0,1:T(4,128)(2,1)S(1)} %get-tuple-element.4), channel_id=1, source_target_pairs={{0,13},{1,0},{4,1},{5,4},{8,5},{9,8},{12,9},{13,12},{2,15},{3,2},{... | collective-permute-start | bytes 49160 | tf_op jit(solution)/shard_map/ppermute | solution.py:53
  31.7 10.0 %all-to-all-start.1 = ((bf16[16,2,1024]{2,0,1:T(8,128)(2,1)}), bf16[16,2,1024]{2,0,1:T(8,128)(2,1)S(1)}, u32[]{:S(2)}, u32[]{:S(2)}) async-start(bf16[16,2,1024]{2,0,1:T(8,128)(2,1)} %bitcast.69), calls=%async_computation.1 | async-start | bytes 131072 | tf_op jit(solution)/shard_map/all_to_all | solution.py:94
  41.6 12.1 %all-to-all-start = ((bf16[8,4,2048]{2,1,0:T(4,128)(2,1)}), bf16[8,4,2048]{2,1,0:T(4,128)(2,1)S(1)}, u32[]{:S(2)}, u32[]{:S(2)}) async-start(bf16[8,4,2048]{2,1,0:T(4,128)(2,1)} %broadcast_select_fusion), calls=%async_computation | async-start | bytes 262144 | tf_op jit(solution)/shard_map/all_to_all | solution.py:79
Sparse Core Ops, SparseCore 0:
  9.5 21.0 all-gather.1
